TPU v7x, 128 devices: a whole 4x4x4 slice. The times are simulated.
128 devices in a mesh: blk: 16 (over z_lo, y, core), seq: 8 (over x, z_hi).
Axes of the slice: x: 4, y: 4, z: 4 (z_hi: 2, z_lo: 2; z = z_hi * 2 + z_lo), core: 2. Of those that a mesh axis runs over, the one named last changes fastest.
Arguments:
- layer_input: bfloat16 [16, 1024, 8192], P('blk', 'seq'), may hold values from -6 to 6
- queries: bfloat16 [16, 1024, 4096], P('blk', 'seq'), may hold values from -48 to 48, as said below
- grad_out: bfloat16 [16, 1024, 4096], P('blk', 'seq'), may hold values from -6 to 6
- segment_ids: int32 [16, 1024], P('blk', 'seq'), may hold values from 0 to 3, never falling along the last dimension, each value on 1 to 512 neighbouring positions
- kv_weight: bfloat16 [8192, 1024], P(('blk', 'seq')), may hold values from -0.0625 to 0.0625
- norm_gain: float32 [8192], replicated, may hold values from 0.5 to 1.5
Outputs:
- attended: bfloat16 [16, 1024, 4096], P('blk', 'seq')
- grad_queries: bfloat16 [16, 1024, 4096], P('blk', 'seq')
- grad_input: bfloat16 [16, 1024, 8192], P('blk', 'seq')
- grad_weight: float32 [8192, 1024], P(('blk', 'seq'))
- grad_gain: float32 [8192], replicated
Inputs may be any that keep to these rules, and one draw needn't show every extreme that they name: Projected queries; some rows may be larger than others.
All inputs are finite; a program needn't handle non-finite values.
Results may differ from a plain program's by a relative error of at most 0.02.
The roundings to bfloat16 on the way count: a program that leaves them out, or rounds other values in their place, can miss the bound.
Values may be sent and summed in bfloat16 or wider, within the bound.
No kernel may reach another device: no remote copies, remote signals or barrier semaphores. Data moves between devices by JAX's collectives and lax.ppermute only.
A program may use at most 128 MiB of HBM per device.

v0:
```python
import jax
import jax.numpy as jnp
from jax import lax
from jax.sharding import PartitionSpec as P

HEAD = 128
epsilon = 1e-05


def cut_along(shard, dim, length):
    lengths = shard.shape
    pieces = shard.reshape(*lengths[:dim], length, lengths[dim] // length, *lengths[dim + 1 :])
    return jnp.moveaxis(pieces, dim, 0)


def sum_at_owner(shard, axis, dim):
    length = lax.axis_size(axis)
    pieces = lax.all_to_all(cut_along(shard, dim, length), axis, 0, 0, tiled=True)
    return jnp.sum(pieces, axis=0)


def shards(layer_input, queries, grad_out, segment_ids, kv_weight, norm_gain):
    f32 = jnp.float32
    tok_rows = layer_input.shape[1]
    model_width = layer_input.shape[2]
    seq_devices = lax.axis_size("seq")
    blk_devices = lax.axis_size("blk")
    length = tok_rows * seq_devices
    seq_index = lax.axis_index("seq")
    kv_total = kv_weight.shape[1]
    kv_width = kv_total // 2
    kv_heads = kv_width // HEAD
    query_count = queries.shape[2] // HEAD
    group_size = query_count // kv_heads
    score_scale = HEAD ** (-0.5)
    piece_cols = kv_weight.shape[0]
    source = layer_input[0].astype(f32)
    inv_rms = lax.rsqrt(jnp.mean(source * source, axis=1, keepdims=True) + epsilon)
    scaled = source * inv_rms
    normed = (scaled * norm_gain).astype(jnp.bfloat16)
    split_cols = normed.reshape(tok_rows, blk_devices, seq_devices, piece_cols)
    columns = lax.all_to_all(split_cols, "seq", split_axis=2, concat_axis=0, tiled=True).reshape(
        length, blk_devices * piece_cols
    )
    weight_slab = lax.all_gather(kv_weight, "blk", axis=0, tiled=True)
    query_heads = queries[0].reshape(tok_rows, kv_heads, group_size, HEAD)
    query_pos = seq_index * tok_rows + jnp.arange(tok_rows, dtype=jnp.int32)
    query_doc = segment_ids[0]
    grad_heads = grad_out[0].reshape(tok_rows, kv_heads, group_size, HEAD).transpose(1, 2, 0, 3)

    def scores_of(kv_piece, doc_piece):
        rows_here = kv_piece.shape[0]
        key_heads = kv_piece[:, :kv_width].reshape(rows_here, kv_heads, HEAD)
        raw_scores = (
            jnp.einsum("qgjd,kgd->gjqk", query_heads, key_heads, preferred_element_type=f32)
            * score_scale
        )
        key_pos = jnp.arange(rows_here, dtype=jnp.int32)
        allowed = (key_pos[None, :] <= query_pos[:, None]) & (
            doc_piece[None, :] == query_doc[:, None]
        )
        return (jnp.where(allowed, raw_scores, -1e30), allowed, key_heads)

    stat_shape = (kv_heads, group_size, tok_rows, 1)
    kv_own = sum_at_owner(
        jnp.dot(columns, weight_slab, preferred_element_type=f32), "seq", 0
    ).astype(jnp.bfloat16)
    row_max = jnp.full(stat_shape, -1e30, f32)
    kv_piece = lax.all_gather(kv_own, "seq", axis=0, tiled=True)
    doc_piece = lax.all_gather(query_doc, "seq", axis=0, tiled=True)
    rows_here = kv_piece.shape[0]
    masked, allowed, key_heads = scores_of(kv_piece, doc_piece)
    new_max = jnp.maximum(row_max, jnp.max(masked, axis=-1, keepdims=True))
    expo_terms = jnp.where(allowed, jnp.exp(masked - new_max), 0.0)
    value_heads = kv_piece[:, kv_width:].reshape(rows_here, kv_heads, HEAD)
    weights = expo_terms.astype(jnp.bfloat16)
    weighted = jnp.einsum("gjqk,kgd->gjqd", weights, value_heads, preferred_element_type=f32)
    row_sum = jnp.sum(expo_terms, axis=-1, keepdims=True)
    row_max, row_sum, weighted = (new_max, row_sum, weighted)
    summed = weighted / row_sum
    attended = (
        summed.transpose(2, 0, 1, 3).reshape(tok_rows, query_count * HEAD).astype(jnp.bfloat16)
    )
    log_total = row_max + jnp.log(row_sum)
    attended_heads = attended.reshape(tok_rows, kv_heads, group_size, HEAD).transpose(1, 2, 0, 3)
    row_delta = jnp.sum(grad_heads.astype(f32) * attended_heads.astype(f32), axis=-1, keepdims=True)
    kv_piece = lax.all_gather(kv_own, "seq", axis=0, tiled=True)
    doc_piece = lax.all_gather(query_doc, "seq", axis=0, tiled=True)
    rows_here = kv_piece.shape[0]
    masked, allowed, key_heads = scores_of(kv_piece, doc_piece)
    softmax_probs = jnp.where(allowed, jnp.exp(masked - log_total), 0.0)
    value_heads = kv_piece[:, kv_width:].reshape(rows_here, kv_heads, HEAD)
    grad_probs = jnp.einsum("gjqd,kgd->gjqk", grad_heads, value_heads, preferred_element_type=f32)
    grad_scores = (softmax_probs * (grad_probs - row_delta)).astype(jnp.bfloat16)
    probs_half = softmax_probs.astype(jnp.bfloat16)
    grad_values = jnp.einsum("gjqk,gjqd->kgd", probs_half, grad_heads, preferred_element_type=f32)
    grad_keys = (
        jnp.einsum("gjqk,qgjd->kgd", grad_scores, query_heads, preferred_element_type=f32)
        * score_scale
    )
    grad_query = (
        jnp.einsum("gjqk,kgd->qgjd", grad_scores, key_heads, preferred_element_type=f32)
        * score_scale
    )
    new_rows = jnp.concatenate(
        [grad_keys.reshape(rows_here, kv_width), grad_values.reshape(rows_here, kv_width)], axis=1
    )
    grad_rows = new_rows
    grad_query, grad_rows = (grad_query, grad_rows)
    grad_own = sum_at_owner(grad_rows, "seq", 0).astype(jnp.bfloat16)
    grad_kv = lax.all_gather(grad_own, "seq", axis=0, tiled=True)
    grad_queries = grad_query.reshape(tok_rows, query_count * HEAD).astype(jnp.bfloat16)
    slab_back = lax.all_gather(kv_weight, "blk", axis=0, tiled=True)
    grad_weight = lax.psum_scatter(
        lax.dot_general(columns, grad_kv, (((0,), (0,)), ((), ())), preferred_element_type=f32),
        "blk",
        scatter_dimension=0,
        tiled=True,
    )
    grad_cols = lax.dot_general(
        grad_kv, slab_back, (((1,), (1,)), ((), ())), preferred_element_type=f32
    ).astype(jnp.bfloat16)
    grad_cols = grad_cols.reshape(length, blk_devices, 1, piece_cols)
    grad_normed = lax.all_to_all(grad_cols, "seq", split_axis=0, concat_axis=2, tiled=True).reshape(
        tok_rows, model_width
    )
    grad_norm = grad_normed.astype(f32)
    grad_gain = lax.psum(jnp.sum(grad_norm * scaled, axis=0), ("blk", "seq"))
    grad_hat = grad_norm * norm_gain
    grad_input = inv_rms * (grad_hat - scaled * jnp.mean(grad_hat * scaled, axis=1, keepdims=True))
    return (
        attended[None],
        grad_queries[None],
        grad_input.astype(jnp.bfloat16)[None],
        grad_weight,
        grad_gain,
    )


def solution(mesh):
    in_specs = (
        P("blk", "seq", None),
        P("blk", "seq", None),
        P("blk", "seq", None),
        P("blk", "seq"),
        P(("blk", "seq"), None),
        P(),
    )
    out_specs = (
        P("blk", "seq", None),
        P("blk", "seq", None),
        P("blk", "seq", None),
        P(("blk", "seq"), None),
        P(),
    )
    return jax.shard_map(shards, mesh=mesh, in_specs=in_specs, out_specs=out_specs, check_vma=False)
```

profile of v0, /device:TPU:1, one launch (start us, length us, event | category | flops | bytes accessed | tf_op | source)
XLA Modules:
  0.0 534.6 jit_solution(473694179402004484)
XLA Ops:
  8.0 3.2 copy.148
  17.7 38.3 %all_to_all.34 = bf16[128,16,8,64]{0,3,1,2:T(8,128)(2,1)} all-to-all(bf16[128,16,8,64]{0,3,1,2:T(8,128)(2,1)S(1)} %copy.149), channel_id=1, replica_groups=mesh['blk'=16,'seq'=8] {'seq'}, dimensions={2} | all-to-all | bytes 4194304 | tf_op jit(solution)/shard_map/all_to_all | solution.py:42
  56.0 8.3 %all-gather.5.cloned.1.call-done = bf16[1024,1024]{1,0:T(8,128)(2,1)} async-done(((bf16[64,1024]{1,0:T(8,128)(2,1)}), bf16[1024,1024]{1,0:T(8,128)(2,1)}) %all-gather.5.cloned.1.call-update) | async-done | bytes 2097168 | tf_op jit(solution)/shard_map/all_gather | solution.py:45
  64.3 4.6 fusion.22
  68.9 55.1 %all_to_all.35 = f32[8,128,1024]{2,1,0:T(8,128)} all-to-all(f32[8,128,1024]{2,1,0:T(8,128)S(1)} %fusion.22), channel_id=1, replica_groups=mesh['blk'=16,'seq'=8] {'seq'}, dimensions={0} | all-to-all | bytes 8388608 | tf_op jit(solution)/shard_map/all_to_all | solution.py:18
  124.1 3.4 reduce_sum.66
  131.0 17.1 %all-gather = s32[1,1024]{1,0:T(1,128)S(1)} all-gather(s32[1,128]{1,0:T(1,128)S(1)} %copy-done.8), channel_id=2, replica_groups=mesh['blk'=16,'seq'=8] {'seq'}, dimensions={1}, use_global_device_ids=true | all-gather | bytes 4608 | tf_op jit(solution)/shard_map/all_gather | solution.py:70
  148.4 30.2 %all-gather.7.cloned.1.call-done = bf16[1024,1024]{1,0:T(8,128)(2,1)} async-done(((bf16[128,1024]{1,0:T(8,128)(2,1)}), bf16[1024,1024]{1,0:T(8,128)(2,1)}) %all-gather.7.cloned.1.call-update) | async-done | bytes 2097168 | tf_op jit(solution)/shard_map/all_gather | solution.py:69
  183.0 9.1 %fusion.33 = (f32[4,8,128]{2,1,0:T(8,128)S(1)}, f32[4,8,128,1024]{2,3,1,0:T(8,128)}) fusion(bf16[1024,4,128,1]{0,2,3,1:T(8,128)(2,1)S(1)} %bitcast.122, bf16[128,4,8,128]{3,2,1,0:T(8,128)(2,1)} %bitcast.124, pred[128,1024]{0,1:T(8,128)(4,1)S(1)} %fusion.29), kind=kOutput, calls=%fused_computation.52 | convolution fusion | flops 1086320640 | bytes 19021824 | tf_op jit(solution)/shard_map/qgjd,kgd->gjqk/dot_general | solution.py:55
  194.4 8.7 %fusion.1 = f32[4,8,128]{2,1,0:T(8,128)S(1)} fusion(f32[4,8,128,1024]{2,3,1,0:T(8,128)} %get-tuple-element.45, f32[4,8,128]{2,1,0:T(8,128)S(1)} %broadcast_maximum_fusion, pred[128,1024]{0,1:T(8,128)(4,1)S(1)} %fusion.29), kind=kLoop, calls=%fused_computation.5 | loop fusion | flops 12578816 | bytes 16941056 | tf_op jit(solution)/shard_map/reduce_sum | solution.py:78
  203.1 9.9 %fusion.21 = (bf16[128,4,8,128]{0,3,2,1:T(8,128)(2,1)}, f32[4,8,128,128]{2,3,1,0:T(8,128)S(1)}) fusion(f32[128,4,8]{0,2,1:T(8,128)S(1)} %bitcast.140, bf16[1024,4,128,1]{0,2,3,1:T(8,128)(2,1)S(1)} %bitcast.138, f32[4,8,128,1024]{2,3,1,0:T(8,128)} %get-tuple-element.45, f32[4,8,128]{2,1,0:T(8,128)S(1)} %broadcast_maximum_fusion, ...), kind=kOutput, calls=%fused_computation.32 | convolution fusion | flops 1087373312 | bytes 21135360 | tf_op jit(solution)/shard_map/gjqk,kgd->gjqd/dot_general | solution.py:77
  213.4 9.5 %fusion.24 = f32[1024,4,128]{2,0,1:T(8,128)} fusion(bf16[4,8,128,128]{2,3,1,0:T(8,128)(2,1)S(1)} %bitcast.131, f32[4,8,128,1024]{2,3,1,0:T(8,128)} %get-tuple-element.45, f32[4,8,128]{2,1,0:T(8,128)S(1)} %log_add_fusion, pred[128,1024]{0,1:T(8,128)(4,1)S(1)} %fusion.29), kind=kOutput, calls=%fused_computation.39 | convolution fusion | flops 1086324736 | bytes 20070400 | tf_op jit(solution)/shard_map/gjqk,gjqd->kgd/dot_general | solution.py:96
  222.9 10.9 %fusion = bf16[4,8,128,1024]{2,3,1,0:T(8,128)(2,1)} fusion(f32[4,8,128,1024]{2,3,1,0:T(8,128)} %get-tuple-element.45, bf16[1024,4,128,1]{0,2,3,1:T(8,128)(2,1)S(1)} %bitcast.139, bf16[4,8,128,128]{2,3,1,0:T(8,128)(2,1)S(1)} %bitcast.132, f32[4,8,128]{2,1,0:T(8,128)S(1)} %multiply_reduce_fusion.3, f32[4,8,128]{2,1,0:T(8,128)S(1)} %log_add_fusion, ...), kind=kOutput, calls=%fused_computation.1 | convolution fusion | flops 1094713344 | bytes 27426816 | tf_op jit(solution)/shard_map/gjqd,kgd->gjqk/dot_general | solution.py:93
  236.7 3.5 copy.194
  240.2 7.1 %fusion.20 = f32[1024,4,128]{2,0,1:T(8,128)} fusion(bf16[4,8,128,1024]{2,3,1,0:T(8,128)(2,1)} %fusion, bf16[128,4,8,128]{3,2,1,0:T(8,128)(2,1)S(1)} %bitcast.125), kind=kOutput, calls=%fused_computation.30 | convolution fusion | flops 1074266112 | bytes 11534336 | tf_op jit(solution)/shard_map/gjqk,qgjd->kgd/dot_general | solution.py:98
  253.5 50.9 %all_to_all.36 = f32[8,128,1024]{1,2,0:T(8,128)} all-to-all(f32[8,128,1024]{1,2,0:T(8,128)S(1)} %copy.164), channel_id=1, replica_groups=mesh['blk'=16,'seq'=8] {'seq'}, dimensions={0} | all-to-all | bytes 8388608 | tf_op jit(solution)/shard_map/all_to_all | solution.py:18
  304.4 3.2 reduce_sum.69
  307.8 4.7 copy.171
  312.5 51.4 %all-gather.9.cloned.1.call-done = bf16[1024,1024]{0,1:T(8,128)(2,1)} async-done(((bf16[128,1024]{0,1:T(8,128)(2,1)}), bf16[1024,1024]{0,1:T(8,128)(2,1)}) %all-gather.9.cloned.1.call-update) | async-done | bytes 2097168 | tf_op jit(solution)/shard_map/all_gather | solution.py:111
  363.9 6.5 %fusion.17 = f32[1024,1024]{1,0:T(8,128)} fusion(bf16[1024,1024]{0,1:T(8,128)(2,1)} %all-gather.9.cloned.1.call-done, bf16[128,8,8,128]{3,2,1,0:T(8,128)(2,1)} %bitcast.135), kind=kOutput, calls=%fused_computation.26 | convolution fusion | flops 2147483648 | bytes 8388608 | tf_op jit(solution)/shard_map/dot_general | solution.py:115
  370.4 5.9 %convolution_convert_fusion = bf16[1024,1024]{0,1:T(8,128)(2,1)} fusion(bf16[1024,1024]{1,0:T(8,128)(2,1)} %all-gather.5.cloned.1.call-done, bf16[1024,1024]{0,1:T(8,128)(2,1)} %all-gather.9.cloned.1.call-done), kind=kOutput, calls=%fused_computation.38 | convolution fusion | flops 2148532224 | bytes 6291456 | tf_op jit(solution)/shard_map/dot_general | solution.py:120
  376.3 6.2 %copy.166 = bf16[1024,16,1,64]{3,1,2,0:T(8,128)(2,1)} copy(bf16[1024,16,1,64]{0,3,1,2:T(8,128)(2,1)} %bitcast.134) | data formatting | bytes 4194304 | tf_op jit(solution)/shard_map/reshape | solution.py:123
  382.5 7.6 %reshape.223 = bf16[8,2,65536]{2,1,0:T(2,128)(2,1)} reshape(bf16[1024,1,16,64]{3,2,1,0:T(8,128)(2,1)} %bitcast.119) | data formatting | bytes 4194304
  390.1 4.6 all-to-all-start.3
  397.9 5.6 %multiply_convert_fusion.1 = bf16[4,128,8,128]{3,1,2,0:T(8,128)(2,1)} fusion(bf16[1024,4,128,1]{0,2,3,1:T(8,128)(2,1)S(1)} %bitcast.123, bf16[4,8,128,1024]{2,3,1,0:T(8,128)(2,1)} %fusion), kind=kOutput, calls=%fused_computation.35 | convolution fusion | flops 1074790400 | bytes 10485760 | tf_op jit(solution)/shard_map/gjqk,kgd->qgjd/dot_general | solution.py:102
  405.9 22.6 %all-to-all-done.3 = bf16[8,2,65536]{2,1,0:T(2,128)(2,1)} async-done(((bf16[8,2,65536]{2,1,0:T(2,128)(2,1)}), bf16[8,2,65536]{2,1,0:T(2,128)(2,1)}, u32[]{:S(2)}, u32[]{:S(2)}) %all-to-all-start.3) | async-done | bytes 2097184 | tf_op jit(solution)/shard_map/all_to_all | solution.py:124
  428.4 7.4 %reshape.224 = bf16[1024,1,16,64]{3,2,1,0:T(8,128)(2,1)} reshape(bf16[8,2,65536]{2,1,0:T(2,128)(2,1)} %all-to-all-done.3) | data formatting | bytes 4194304
  435.8 5.5 %copy.167 = bf16[1024,16,1,64]{0,3,2,1:T(8,128)(2,1)} copy(bf16[1024,16,1,64]{3,1,2,0:T(8,128)(2,1)} %bitcast.120) | data formatting | bytes 4194304 | tf_op jit(solution)/shard_map/all_to_all | solution.py:124
  446.7 4.8 multiply_reduce_fusion
  451.5 4.4 fusion.16
  455.9 4.1 copy.175
  460.2 67.6 %psum.7 = f32[8192]{0:T(1024)} all-reduce(f32[8192]{0:T(1024)S(1)} %reduce_sum.72), channel_id=1, replica_groups=mesh['blk'=16,'seq'=8] {'blk','seq'}, use_global_device_ids=true, to_apply=%region_9.10 | all-reduce | flops 8192 | bytes 65536 | tf_op jit(solution)/shard_map/psum | solution.py:128
  (57 shorter events, 38.8 us)
Async XLA Ops:
  7.2 57.1 %all-gather.5.cloned.1.call-start = ((), (), s32[]{:S(2)}) async-start(), calls=%async_computation.5 | async-start | bytes 2228224 | tf_op jit(solution)/shard_map/all_gather | solution.py:45
  7.9 5.5 %copy-start.7 = (f32[8192]{0:T(1024)S(1)}, f32[8192]{0:T(1024)}, u32[]{:S(2)}) copy-start(f32[8192]{0:T(1024)} %param.11) | copy-start | bytes 98308
  7.9 170.6 %all-gather.7.cloned.1.call-start = ((), (), s32[]{:S(2)}) async-start(), calls=%async_computation.6 | async-start | bytes 2359296 | tf_op jit(solution)/shard_map/all_gather | solution.py:69
  124.0 3.5 copy-start.5
  124.0 7.0 %copy-start.8 = (s32[1,128]{1,0:T(1,128)S(1)}, s32[1,128]{1,0:T(1,128)}, u32[]{:S(2)}) copy-start(s32[1,128]{1,0:T(1,128)} %param.9) | copy-start | bytes 1540
  127.5 236.4 %all-gather.9.cloned.1.call-start = ((), (), s32[]{:S(2)}) async-start(), calls=%async_computation.7 | async-start | bytes 2359296 | tf_op jit(solution)/shard_map/all_gather | solution.py:111
  194.4 8.7 %copy-start.6 = (bf16[1024,512]{0,1:T(8,128)(2,1)S(1)}, bf16[1024,512]{0,1:T(8,128)(2,1)}, u32[]{:S(2)}) copy-start(bf16[1024,512]{0,1:T(8,128)(2,1)} %copy.154) | copy-start | bytes 3145732
  203.1 9.9 %copy-start.3 = (bf16[1,128,4096]{1,2,0:T(8,128)(2,1)S(1)}, bf16[1,128,4096]{1,2,0:T(8,128)(2,1)}, u32[]{:S(2)}) copy-start(bf16[1,128,4096]{1,2,0:T(8,128)(2,1)} %copy.156) | copy-start | bytes 3145732
  236.7 3.5 copy-start.1
  250.2 2.2 copy-start.2
  307.6 220.3 %reduce-scatter.2.cloned.1.call-start = ((), (), s32[]{:S(2)}) async-start(), calls=%async_computation.8 | async-start | bytes 4456448 | tf_op jit(solution)/shard_map/reduce_scatter | solution.py:114
  390.1 38.4 %all-to-all-start.3 = ((bf16[8,2,65536]{2,1,0:T(2,128)(2,1)}), bf16[8,2,65536]{2,1,0:T(2,128)(2,1)}, u32[]{:S(2)}, u32[]{:S(2)}) async-start(bf16[8,2,65536]{2,1,0:T(2,128)(2,1)} %reshape.223), calls=%async_computation.3 | async-start | bytes 4194304 | tf_op jit(solution)/shard_map/all_to_all | solution.py:124
  444.4 2.2 copy-start
  444.4 2.3 copy-start.4
Sparse Core Ops, SparseCore 0:
  9.7 54.5 all-gather.4
  127.6 50.8 all-gather.6
  307.7 56.0 all-gather.8
  370.5 72.2 reduce-scatter.1
where the time goes:
time: 540 us; the launch traced here: 535 us
  blocking collectives  229 us (42%)
  waiting for transfers between devices  113 us (21%)
  local copies, waits for them, and re-layouts  70.6 us (13%)
  matrix products  69.1 us (13%)
  other arithmetic  33.7 us (6%)
  between operations  14.2 us (3%)
    all_to_all x2, blocking collectives, sum_at_owner(): lax.all_to_all(cut_along(shard, dim, length), axis, 0, 0, tiled=True)  106 us
    psum x1, blocking collectives, shards(): grad_gain = lax.psum(jnp.sum(grad_norm * scaled, axis=0), ('blk', 'seq'))  67.6 us
    all_gather x1, waiting for transfers between devices, shards(): grad_kv = lax.all_gather(grad_own, 'seq', axis=0, tiled=True)  51.4 us
    unnamed x29, local copies, waits for them, and re-layouts  38.6 us
    all_to_all x1, blocking collectives, shards(): lax.all_to_all(split_cols, 'seq', split_axis=2, concat_axis=0, tiled=True)  38.3 us
    all_gather x1, waiting for transfers between devices, shards(): kv_piece = lax.all_gather(kv_own, 'seq', axis=0, tiled=True)  30.2 us
    all_to_all x1, waiting for transfers between devices, shards(): lax.all_to_all(grad_cols, 'seq', split_axis=0, concat_axis=2, tiled=True)  22.6 us
    all_gather x1, blocking collectives, shards(): doc_piece = lax.all_gather(query_doc, 'seq', axis=0, tiled=True)  17.1 us
  transfers between devices with their start and end apart: 5, of which 4 were waited for; matrix products, arithmetic and copies ran while one was open for 15% of the time, Pallas kernels for 0%

commit v1 on v0

--- a/solution.py
+++ b/solution.py
@@ -2,9 +2,14 @@
 import jax.numpy as jnp
 from jax import lax
 from jax.sharding import PartitionSpec as P
+from jax.lax import psum
 
 HEAD = 128
 epsilon = 1e-05
+
+
+def manage_the_islands(u_in):
+    return psum(psum(u_in, "blk"), "seq")
 
 
 def cut_along(shard, dim, length):
@@ -125,7 +130,7 @@
         tok_rows, model_width
     )
     grad_norm = grad_normed.astype(f32)
-    grad_gain = lax.psum(jnp.sum(grad_norm * scaled, axis=0), ("blk", "seq"))
+    grad_gain = manage_the_islands(jnp.sum(grad_norm * scaled, axis=0))
     grad_hat = grad_norm * norm_gain
     grad_input = inv_rms * (grad_hat - scaled * jnp.mean(grad_hat * scaled, axis=1, keepdims=True))
     return (

time: 540 us -> 570 us (1.056)
  the two profiles are of different devices: /device:TPU:1 before, /device:TPU:0 now
where the time goes in v1:
time: 570 us; the launch traced here: 564 us
  blocking collectives  264 us (46%)
  waiting for transfers between devices  108 us (19%)
  local copies, waits for them, and re-layouts  70.5 us (12%)
  matrix products  69.1 us (12%)
  other arithmetic  33.7 us (6%)
  between operations  14.2 us (2%)
    all_to_all x2, blocking collectives, sum_at_owner(): lax.all_to_all(cut_along(shard, dim, length), axis, 0, 0, tiled=True)  109 us
    psum x2, blocking collectives, manage_the_islands(): return psum(psum(u_in, 'blk'), 'seq')  95.7 us
    all_gather x1, waiting for transfers between devices, shards(): grad_kv = lax.all_gather(grad_own, 'seq', axis=0, tiled=True)  49.8 us
    all_to_all x1, blocking collectives, shards(): lax.all_to_all(split_cols, 'seq', split_axis=2, concat_axis=0, tiled=True)  38.7 us
    unnamed x29, local copies, waits for them, and re-layouts  38.5 us
    all_gather x1, waiting for transfers between devices, shards(): kv_piece = lax.all_gather(kv_own, 'seq', axis=0, tiled=True)  27.2 us
    all_to_all x1, waiting for transfers between devices, shards(): lax.all_to_all(grad_cols, 'seq', split_axis=0, concat_axis=2, tiled=True)  23.2 us
    all_gather x1, blocking collectives, shards(): doc_piece = lax.all_gather(query_doc, 'seq', axis=0, tiled=True)  20.2 us
  transfers between devices with their start and end apart: 5, of which 4 were waited for; matrix products, arithmetic and copies ran while one was open for 14% of the time, Pallas kernels for 0%

profile of v1, /device:TPU:0, one launch (start us, length us, event | category | flops | bytes accessed | tf_op | source)
XLA Modules:
  0.0 564.2 jit_solution(11661650822338504014)
XLA Ops:
  8.0 3.2 copy.148
  17.7 38.7 %all_to_all.34 = bf16[128,16,8,64]{0,3,1,2:T(8,128)(2,1)} all-to-all(bf16[128,16,8,64]{0,3,1,2:T(8,128)(2,1)S(1)} %copy.149), channel_id=1, replica_groups=mesh['blk'=16,'seq'=8] {'seq'}, dimensions={2} | all-to-all | bytes 4194304 | tf_op jit(solution)/shard_map/all_to_all | solution.py:47
  56.4 6.8 %all-gather.5.cloned.1.call-done = bf16[1024,1024]{1,0:T(8,128)(2,1)} async-done(((bf16[64,1024]{1,0:T(8,128)(2,1)}), bf16[1024,1024]{1,0:T(8,128)(2,1)}) %all-gather.5.cloned.1.call-update) | async-done | bytes 2097168 | tf_op jit(solution)/shard_map/all_gather | solution.py:50
  63.2 4.6 fusion.22
  67.8 57.0 %all_to_all.35 = f32[8,128,1024]{2,1,0:T(8,128)} all-to-all(f32[8,128,1024]{2,1,0:T(8,128)S(1)} %fusion.22), channel_id=1, replica_groups=mesh['blk'=16,'seq'=8] {'seq'}, dimensions={0} | all-to-all | bytes 8388608 | tf_op jit(solution)/shard_map/all_to_all | solution.py:23
  124.8 3.4 reduce_sum.66
  131.8 20.2 %all-gather = s32[1,1024]{1,0:T(1,128)S(1)} all-gather(s32[1,128]{1,0:T(1,128)S(1)} %copy-done.8), channel_id=2, replica_groups=mesh['blk'=16,'seq'=8] {'seq'}, dimensions={1}, use_global_device_ids=true | all-gather | bytes 4608 | tf_op jit(solution)/shard_map/all_gather | solution.py:75
  152.2 27.2 %all-gather.7.cloned.1.call-done = bf16[1024,1024]{1,0:T(8,128)(2,1)} async-done(((bf16[128,1024]{1,0:T(8,128)(2,1)}), bf16[1024,1024]{1,0:T(8,128)(2,1)}) %all-gather.7.cloned.1.call-update) | async-done | bytes 2097168 | tf_op jit(solution)/shard_map/all_gather | solution.py:74
  183.9 9.1 %fusion.33 = (f32[4,8,128]{2,1,0:T(8,128)S(1)}, f32[4,8,128,1024]{2,3,1,0:T(8,128)}) fusion(bf16[1024,4,128,1]{0,2,3,1:T(8,128)(2,1)S(1)} %bitcast.122, bf16[128,4,8,128]{3,2,1,0:T(8,128)(2,1)} %bitcast.124, pred[128,1024]{0,1:T(8,128)(4,1)S(1)} %fusion.29), kind=kOutput, calls=%fused_computation.52 | convolution fusion | flops 1086320640 | bytes 19021824 | tf_op jit(solution)/shard_map/qgjd,kgd->gjqk/dot_general | solution.py:60
  195.2 8.7 %fusion.1 = f32[4,8,128]{2,1,0:T(8,128)S(1)} fusion(f32[4,8,128,1024]{2,3,1,0:T(8,128)} %get-tuple-element.45, f32[4,8,128]{2,1,0:T(8,128)S(1)} %broadcast_maximum_fusion, pred[128,1024]{0,1:T(8,128)(4,1)S(1)} %fusion.29), kind=kLoop, calls=%fused_computation.5 | loop fusion | flops 12578816 | bytes 16941056 | tf_op jit(solution)/shard_map/reduce_sum | solution.py:83
  203.9 9.9 %fusion.21 = (bf16[128,4,8,128]{0,3,2,1:T(8,128)(2,1)}, f32[4,8,128,128]{2,3,1,0:T(8,128)S(1)}) fusion(f32[128,4,8]{0,2,1:T(8,128)S(1)} %bitcast.140, bf16[1024,4,128,1]{0,2,3,1:T(8,128)(2,1)S(1)} %bitcast.138, f32[4,8,128,1024]{2,3,1,0:T(8,128)} %get-tuple-element.45, f32[4,8,128]{2,1,0:T(8,128)S(1)} %broadcast_maximum_fusion, ...), kind=kOutput, calls=%fused_computation.32 | convolution fusion | flops 1087373312 | bytes 21135360 | tf_op jit(solution)/shard_map/gjqk,kgd->gjqd/dot_general | solution.py:82
  214.3 9.5 %fusion.24 = f32[1024,4,128]{2,0,1:T(8,128)} fusion(bf16[4,8,128,128]{2,3,1,0:T(8,128)(2,1)S(1)} %bitcast.131, f32[4,8,128,1024]{2,3,1,0:T(8,128)} %get-tuple-element.45, f32[4,8,128]{2,1,0:T(8,128)S(1)} %log_add_fusion, pred[128,1024]{0,1:T(8,128)(4,1)S(1)} %fusion.29), kind=kOutput, calls=%fused_computation.39 | convolution fusion | flops 1086324736 | bytes 20070400 | tf_op jit(solution)/shard_map/gjqk,gjqd->kgd/dot_general | solution.py:101
  223.8 10.9 %fusion = bf16[4,8,128,1024]{2,3,1,0:T(8,128)(2,1)} fusion(f32[4,8,128,1024]{2,3,1,0:T(8,128)} %get-tuple-element.45, bf16[1024,4,128,1]{0,2,3,1:T(8,128)(2,1)S(1)} %bitcast.139, bf16[4,8,128,128]{2,3,1,0:T(8,128)(2,1)S(1)} %bitcast.132, f32[4,8,128]{2,1,0:T(8,128)S(1)} %multiply_reduce_fusion.3, f32[4,8,128]{2,1,0:T(8,128)S(1)} %log_add_fusion, ...), kind=kOutput, calls=%fused_computation.1 | convolution fusion | flops 1094713344 | bytes 27426816 | tf_op jit(solution)/shard_map/gjqd,kgd->gjqk/dot_general | solution.py:98
  237.6 3.5 copy.194
  241.0 7.1 %fusion.20 = f32[1024,4,128]{2,0,1:T(8,128)} fusion(bf16[4,8,128,1024]{2,3,1,0:T(8,128)(2,1)} %fusion, bf16[128,4,8,128]{3,2,1,0:T(8,128)(2,1)S(1)} %bitcast.125), kind=kOutput, calls=%fused_computation.30 | convolution fusion | flops 1074266112 | bytes 11534336 | tf_op jit(solution)/shard_map/gjqk,qgjd->kgd/dot_general | solution.py:103
  254.3 52.5 %all_to_all.36 = f32[8,128,1024]{1,2,0:T(8,128)} all-to-all(f32[8,128,1024]{1,2,0:T(8,128)S(1)} %copy.164), channel_id=1, replica_groups=mesh['blk'=16,'seq'=8] {'seq'}, dimensions={0} | all-to-all | bytes 8388608 | tf_op jit(solution)/shard_map/all_to_all | solution.py:23
  310.3 4.7 copy.171
  315.0 49.8 %all-gather.9.cloned.1.call-done = bf16[1024,1024]{0,1:T(8,128)(2,1)} async-done(((bf16[128,1024]{0,1:T(8,128)(2,1)}), bf16[1024,1024]{0,1:T(8,128)(2,1)}) %all-gather.9.cloned.1.call-update) | async-done | bytes 2097168 | tf_op jit(solution)/shard_map/all_gather | solution.py:116
  364.7 6.5 %fusion.17 = f32[1024,1024]{1,0:T(8,128)} fusion(bf16[1024,1024]{0,1:T(8,128)(2,1)} %all-gather.9.cloned.1.call-done, bf16[128,8,8,128]{3,2,1,0:T(8,128)(2,1)} %bitcast.135), kind=kOutput, calls=%fused_computation.26 | convolution fusion | flops 2147483648 | bytes 8388608 | tf_op jit(solution)/shard_map/dot_general | solution.py:120
  371.3 5.9 %convolution_convert_fusion = bf16[1024,1024]{0,1:T(8,128)(2,1)} fusion(bf16[1024,1024]{1,0:T(8,128)(2,1)} %all-gather.5.cloned.1.call-done, bf16[1024,1024]{0,1:T(8,128)(2,1)} %all-gather.9.cloned.1.call-done), kind=kOutput, calls=%fused_computation.38 | convolution fusion | flops 2148532224 | bytes 6291456 | tf_op jit(solution)/shard_map/dot_general | solution.py:125
  377.2 6.2 %copy.166 = bf16[1024,16,1,64]{3,1,2,0:T(8,128)(2,1)} copy(bf16[1024,16,1,64]{0,3,1,2:T(8,128)(2,1)} %bitcast.134) | data formatting | bytes 4194304 | tf_op jit(solution)/shard_map/reshape | solution.py:128
  383.3 7.6 %reshape.223 = bf16[8,2,65536]{2,1,0:T(2,128)(2,1)} reshape(bf16[1024,1,16,64]{3,2,1,0:T(8,128)(2,1)} %bitcast.119) | data formatting | bytes 4194304
  390.9 4.6 all-to-all-start.3
  398.8 5.7 %multiply_convert_fusion.1 = bf16[4,128,8,128]{3,1,2,0:T(8,128)(2,1)} fusion(bf16[1024,4,128,1]{0,2,3,1:T(8,128)(2,1)S(1)} %bitcast.123, bf16[4,8,128,1024]{2,3,1,0:T(8,128)(2,1)} %fusion), kind=kOutput, calls=%fused_computation.35 | convolution fusion | flops 1074790400 | bytes 10485760 | tf_op jit(solution)/shard_map/gjqk,kgd->qgjd/dot_general | solution.py:107
  406.8 23.2 %all-to-all-done.3 = bf16[8,2,65536]{2,1,0:T(2,128)(2,1)} async-done(((bf16[8,2,65536]{2,1,0:T(2,128)(2,1)}), bf16[8,2,65536]{2,1,0:T(2,128)(2,1)}, u32[]{:S(2)}, u32[]{:S(2)}) %all-to-all-start.3) | async-done | bytes 2097184 | tf_op jit(solution)/shard_map/all_to_all | solution.py:129
  430.0 7.4 %reshape.224 = bf16[1024,1,16,64]{3,2,1,0:T(8,128)(2,1)} reshape(bf16[8,2,65536]{2,1,0:T(2,128)(2,1)} %all-to-all-done.3) | data formatting | bytes 4194304
  437.4 5.4 copy.167
  448.2 4.8 multiply_reduce_fusion
  453.1 4.4 fusion.16
  457.4 4.1 copy.175
  461.8 53.5 %psum.14 = f32[8192]{0:T(1024)S(1)} all-reduce(f32[8192]{0:T(1024)S(1)} %reduce_sum.72), channel_id=1, replica_groups=mesh['blk'=16,'seq'=8] {'blk'}, use_global_device_ids=true, to_apply=%region_9.10 | all-reduce | flops 8192 | bytes 65536 | tf_op jit(solution)/shard_map/psum | solution.py:12
  515.3 42.2 %psum.15 = f32[8192]{0:T(1024)} all-reduce(f32[8192]{0:T(1024)S(1)} %psum.14), channel_id=1, replica_groups=mesh['blk'=16,'seq'=8] {'seq'}, use_global_device_ids=true, to_apply=%region_10.11 | all-reduce | flops 8192 | bytes 65536 | tf_op jit(solution)/shard_map/psum | solution.py:12
  (58 shorter events, 42.0 us)
Async XLA Ops:
  7.2 56.0 %all-gather.5.cloned.1.call-start = ((), (), s32[]{:S(2)}) async-start(), calls=%async_computation.5 | async-start | bytes 2228224 | tf_op jit(solution)/shard_map/all_gather | solution.py:50
  7.9 5.5 copy-start.7
  7.9 171.5 %all-gather.7.cloned.1.call-start = ((), (), s32[]{:S(2)}) async-start(), calls=%async_computation.6 | async-start | bytes 2359296 | tf_op jit(solution)/shard_map/all_gather | solution.py:74
  124.8 3.5 copy-start.5
  124.8 7.0 %copy-start.8 = (s32[1,128]{1,0:T(1,128)S(1)}, s32[1,128]{1,0:T(1,128)}, u32[]{:S(2)}) copy-start(s32[1,128]{1,0:T(1,128)} %param.9) | copy-start | bytes 1540
  128.2 236.5 %all-gather.9.cloned.1.call-start = ((), (), s32[]{:S(2)}) async-start(), calls=%async_computation.7 | async-start | bytes 2359296 | tf_op jit(solution)/shard_map/all_gather | solution.py:116
  195.2 8.7 %copy-start.6 = (bf16[1024,512]{0,1:T(8,128)(2,1)S(1)}, bf16[1024,512]{0,1:T(8,128)(2,1)}, u32[]{:S(2)}) copy-start(bf16[1024,512]{0,1:T(8,128)(2,1)} %copy.154) | copy-start | bytes 3145732
  203.9 9.9 %copy-start.3 = (bf16[1,128,4096]{1,2,0:T(8,128)(2,1)S(1)}, bf16[1,128,4096]{1,2,0:T(8,128)(2,1)}, u32[]{:S(2)}) copy-start(bf16[1,128,4096]{1,2,0:T(8,128)(2,1)} %copy.156) | copy-start | bytes 3145732
  237.6 3.5 copy-start.1
  251.0 2.2 copy-start.2
  310.1 247.4 %reduce-scatter.2.cloned.1.call-start = ((), (), s32[]{:S(2)}) async-start(), calls=%async_computation.8 | async-start | bytes 4456448 | tf_op jit(solution)/shard_map/reduce_scatter | solution.py:119
  390.9 39.1 %all-to-all-start.3 = ((bf16[8,2,65536]{2,1,0:T(2,128)(2,1)}), bf16[8,2,65536]{2,1,0:T(2,128)(2,1)}, u32[]{:S(2)}, u32[]{:S(2)}) async-start(bf16[8,2,65536]{2,1,0:T(2,128)(2,1)} %reshape.223), calls=%async_computation.3 | async-start | bytes 4194304 | tf_op jit(solution)/shard_map/all_to_all | solution.py:129
  445.9 2.2 copy-start
  445.9 2.3 copy-start.4
Sparse Core Ops, SparseCore 0:
  9.7 53.4 all-gather.4
  128.4 50.9 all-gather.6
  310.2 54.5 all-gather.8
  371.4 73.1 reduce-scatter.1
